TPU v7x, 32 devices: a whole 2x2x4 slice. The times are simulated.
32 devices in a mesh: dp: 8 (over z, x), tensor: 4 (over y, core).
Axes of the slice: x: 2, y: 2, z: 4, core: 2. Of those that a mesh axis runs over, the one named last changes fastest.
Arguments:
- tokens: bfloat16 [20480, 768], P(('dp', 'tensor')), may hold values from -6 to 6
- cotangent: bfloat16 [20480, 768], P(('dp', 'tensor')), may hold values from -6 to 6
- lengths: int32 [8, 8], P('dp'), may hold values from 1 to 512, 2048 in all within a row
- w_qkv: bfloat16 [768, 3, 768], P('dp', None, 'tensor'), may hold values from -0.21875 to 0.21875
- w_out: bfloat16 [768, 768], P('tensor', 'dp'), may hold values from -6 to 6
- w_fc: bfloat16 [768, 3072], P('dp', 'tensor'), may hold values from -0.21875 to 0.21875
- w_proj: bfloat16 [3072, 768], P('tensor', 'dp'), may hold values from -0.109375 to 0.109375
- ln1_gain: bfloat16 [768], P('dp'), may hold values from 0.25 to 1.75
- ln1_bias: bfloat16 [768], P('dp'), may hold values from -3 to 3
- ln2_gain: bfloat16 [768], P('dp'), may hold values from 0.25 to 1.75
- ln2_bias: bfloat16 [768], P('dp'), may hold values from -3 to 3
Outputs:
- block_out: bfloat16 [20480, 768], P(('dp', 'tensor'))
- input_grad: bfloat16 [20480, 768], P(('dp', 'tensor'))
- w_qkv_grad: float32 [768, 3, 768], P('dp', None, 'tensor')
- w_out_grad: float32 [768, 768], P('tensor', 'dp')
- w_fc_grad: float32 [768, 3072], P('dp', 'tensor')
- w_proj_grad: float32 [3072, 768], P('tensor', 'dp')
- ln1_gain_grad: float32 [768], P('dp')
- ln1_bias_grad: float32 [768], P('dp')
- ln2_gain_grad: float32 [768], P('dp')
- ln2_bias_grad: float32 [768], P('dp')
Inputs may be any that keep to these rules, and one draw needn't show every extreme that they name: `lengths`: row g lists the token counts of group g's 8 continuations in order after its 512-token prompt; each row sums to 2048 and its largest entry is exactly 512.
All inputs are finite; a program needn't handle non-finite values.
Results may differ from a plain program's by a relative error of at most 0.019.
The roundings to bfloat16 on the way count: a program that leaves them out, or rounds other values in their place, can miss the bound.
Values may be sent and summed in bfloat16 or wider, within the bound.
A program may use at most 192 MiB of HBM per device.

v0:
```python
import jax
import jax.numpy as jnp
from jax import lax
from jax.sharding import PartitionSpec as P

HEAD = 64
PROMPT = 512


def normalize(values):
    mean = jnp.mean(values, axis=-1, keepdims=True)
    centred = values - mean
    spread = jnp.mean(centred * centred, axis=-1, keepdims=True)
    factor = lax.rsqrt(spread + 1e-05)
    return (centred * factor, factor)


def norm_back(grad_out, normed, factor, gain):
    scaled = grad_out * gain
    first = jnp.mean(scaled, axis=-1, keepdims=True)
    second = jnp.mean(scaled * normed, axis=-1, keepdims=True)
    return factor * (scaled - first - normed * second)


def gelu_tanh(values):
    return jax.nn.gelu(values, approximate=True)


def inner_rows(left, right):
    return lax.dot_general(
        left, right, (((0,), (0,)), ((), ())), preferred_element_type=jnp.float32
    )


def times_trans(left, right):
    return lax.dot_general(
        left, right, (((1,), (1,)), ((), ())), preferred_element_type=jnp.float32
    )


def segment_ids(lengths, total):
    ends = PROMPT + jnp.cumsum(lengths[0])
    places = jnp.arange(total, dtype=jnp.int32)
    passed = jnp.sum((places[:, None] >= ends[None, :]).astype(jnp.int32), axis=1)
    return (places, jnp.where(places < PROMPT, -1, passed))


def visible(query_pos, query_seg, key_pos, key_seg):
    causal = key_pos[None, :] <= query_pos[:, None]
    shared = (key_seg[None, :] < 0) | (key_seg[None, :] == query_seg[:, None])
    return (causal & shared)[None]


def attend(queries, keys, values, places, segs, block, scale):
    count = queries.shape[0] // block

    def one(index):
        start = index * block
        query = lax.dynamic_slice_in_dim(queries, start, block, 0)
        mask = visible(
            lax.dynamic_slice_in_dim(places, start, block, 0),
            lax.dynamic_slice_in_dim(segs, start, block, 0),
            places,
            segs,
        )
        raw = jnp.einsum("qhd,khd->hqk", query, keys, preferred_element_type=jnp.float32) * scale
        magnitude = jnp.where(mask, jnp.abs(raw), -1e30)
        top = jnp.max(magnitude, axis=-1, keepdims=True)
        expo = jnp.where(mask, jnp.exp(magnitude - top), 0.0)
        total = jnp.sum(expo, axis=-1, keepdims=True)
        weights = (jnp.sign(raw) * (expo / total)).astype(jnp.bfloat16)
        mixed = jnp.einsum("hqk,khd->qhd", weights, values, preferred_element_type=jnp.float32)
        return (mixed.astype(jnp.bfloat16), (top + jnp.log(total))[..., 0])

    mixed, sums = lax.map(one, jnp.arange(count, dtype=jnp.int32))
    return (mixed.reshape(queries.shape[0], -1), sums)


def attend_back(queries, keys, values, grad_mixed, sums, places, segs, block, scale):
    count = queries.shape[0] // block

    def step(carry, inputs):
        key_grad, value_grad = carry
        index, lse_block = inputs
        start = index * block
        query = lax.dynamic_slice_in_dim(queries, start, block, 0)
        grad_block = lax.dynamic_slice_in_dim(grad_mixed, start, block, 0)
        mask = visible(
            lax.dynamic_slice_in_dim(places, start, block, 0),
            lax.dynamic_slice_in_dim(segs, start, block, 0),
            places,
            segs,
        )
        raw = jnp.einsum("qhd,khd->hqk", query, keys, preferred_element_type=jnp.float32) * scale
        prob = jnp.where(mask, jnp.exp(jnp.abs(raw) - lse_block[..., None]), 0.0)
        signed = jnp.sign(raw) * prob
        rounded = signed.astype(jnp.bfloat16)
        value_grad = value_grad + jnp.einsum(
            "hqk,qhd->khd", rounded, grad_block, preferred_element_type=jnp.float32
        )
        weight_grad = jnp.einsum(
            "qhd,khd->hqk", grad_block, values, preferred_element_type=jnp.float32
        )
        inner = jnp.sum(signed * weight_grad, axis=-1, keepdims=True)
        score_grad = (prob * weight_grad - signed * inner).astype(jnp.bfloat16)
        query_grad = (
            jnp.einsum("hqk,khd->qhd", score_grad, keys, preferred_element_type=jnp.float32) * scale
        )
        key_grad = (
            key_grad
            + jnp.einsum("hqk,qhd->khd", score_grad, query, preferred_element_type=jnp.float32)
            * scale
        )
        return ((key_grad, value_grad), query_grad)

    zeros = jnp.zeros(keys.shape, jnp.float32)
    (key_grad, value_grad), query_grad = lax.scan(
        step, (zeros, zeros), (jnp.arange(count, dtype=jnp.int32), sums)
    )
    return (query_grad.reshape(keys.shape), key_grad, value_grad)


def on_device(
    tokens, cotangent, lengths, w_qkv, w_out, w_fc, w_proj, ln1_gain, ln1_bias, ln2_gain, ln2_bias
):
    rows = tokens.shape[0]
    group = rows * lax.axis_size("tensor")
    block = group // max(1, group // 512)
    scale = HEAD ** (-0.5)
    pieces = (w_qkv, w_out, w_fc, w_proj, ln1_gain, ln1_bias, ln2_gain, ln2_bias)
    qkv_full, out_full, fc_full, proj_full, gain1, bias1, gain2, bias2 = (
        lax.all_gather(pieces[0], "dp", axis=0, tiled=True),
        lax.all_gather(pieces[1], "dp", axis=1, tiled=True),
        lax.all_gather(pieces[2], "dp", axis=0, tiled=True),
        lax.all_gather(pieces[3], "dp", axis=1, tiled=True),
        lax.all_gather(pieces[4], "dp", axis=0, tiled=True),
        lax.all_gather(pieces[5], "dp", axis=0, tiled=True),
        lax.all_gather(pieces[6], "dp", axis=0, tiled=True),
        lax.all_gather(pieces[7], "dp", axis=0, tiled=True),
    )
    gain1 = gain1.astype(jnp.float32)
    bias1 = bias1.astype(jnp.float32)
    gain2 = gain2.astype(jnp.float32)
    bias2 = bias2.astype(jnp.float32)
    width = qkv_full.shape[0]
    local = qkv_full.shape[2]
    heads = local // HEAD
    qkv_mat = qkv_full.reshape(width, 3 * local)
    places, segs = segment_ids(lengths, group)
    inputs = tokens.astype(jnp.float32)
    normed1, factor1 = normalize(inputs)
    lowered1 = (normed1 * gain1 + bias1).astype(jnp.bfloat16)
    all_norm1 = lax.all_gather(lowered1, "tensor", axis=0, tiled=True)
    projected = jnp.dot(all_norm1, qkv_mat, preferred_element_type=jnp.float32).astype(jnp.bfloat16)
    projected = projected.reshape(group, 3, heads, HEAD)
    queries = projected[:, 0]
    keys = projected[:, 1]
    values = projected[:, 2]
    mixed, sums = attend(queries, keys, values, places, segs, block, scale)
    part = mixed
    resid = inputs + lax.psum_scatter(
        jnp.dot(part, out_full, preferred_element_type=jnp.float32).astype(jnp.bfloat16),
        "tensor",
        scatter_dimension=0,
        tiled=True,
    ).astype(jnp.float32)
    normed2, factor2 = normalize(resid)
    lowered2 = (normed2 * gain2 + bias2).astype(jnp.bfloat16)
    all_norm2 = lax.all_gather(lowered2, "tensor", axis=0, tiled=True)
    hidden_pre = jnp.dot(all_norm2, fc_full, preferred_element_type=jnp.float32)
    hidden, gelu_pull = jax.vjp(gelu_tanh, hidden_pre)
    hidden_low = hidden.astype(jnp.bfloat16)
    part = hidden_low
    mlp_rows = lax.psum_scatter(
        jnp.dot(part, proj_full, preferred_element_type=jnp.float32).astype(jnp.bfloat16),
        "tensor",
        scatter_dimension=0,
        tiled=True,
    ).astype(jnp.float32)
    block_out = (resid + mlp_rows).astype(jnp.bfloat16)
    grad_all = lax.all_gather(cotangent, "tensor", axis=0, tiled=True)
    hidden_grad = times_trans(grad_all, proj_full)
    proj_grad = inner_rows(hidden_low, grad_all)
    pre_low = gelu_pull(hidden_grad)[0].astype(jnp.bfloat16)
    fc_grad = inner_rows(all_norm2, pre_low)
    part = pre_low
    norm2_grad = lax.psum_scatter(
        times_trans(part, fc_full).astype(jnp.bfloat16), "tensor", scatter_dimension=0, tiled=True
    ).astype(jnp.float32)
    gain2_part = jnp.sum(norm2_grad * normed2, axis=0)
    bias2_part = jnp.sum(norm2_grad, axis=0)
    resid_grad = cotangent.astype(jnp.float32) + norm_back(norm2_grad, normed2, factor2, gain2)
    resid_low = resid_grad.astype(jnp.bfloat16)
    resid_all = lax.all_gather(resid_low, "tensor", axis=0, tiled=True)
    out_grad = inner_rows(mixed, resid_all)
    mixed_grad = times_trans(resid_all, out_full).astype(jnp.bfloat16).reshape(group, heads, HEAD)
    query_grad, key_grad, value_grad = attend_back(
        queries, keys, values, mixed_grad, sums, places, segs, block, scale
    )
    qkv_grad_low = (
        jnp.stack([query_grad, key_grad, value_grad], axis=1)
        .astype(jnp.bfloat16)
        .reshape(group, 3 * local)
    )
    qkv_grad = inner_rows(all_norm1, qkv_grad_low).reshape(width, 3, local)
    part = qkv_grad_low
    norm1_grad = lax.psum_scatter(
        times_trans(part, qkv_mat).astype(jnp.bfloat16), "tensor", scatter_dimension=0, tiled=True
    ).astype(jnp.float32)
    gain1_part = jnp.sum(norm1_grad * normed1, axis=0)
    bias1_part = jnp.sum(norm1_grad, axis=0)
    input_grad = (resid_grad + norm_back(norm1_grad, normed1, factor1, gain1)).astype(jnp.bfloat16)
    qkv_sum, out_sum, fc_sum, proj_sum, gain1_share, bias1_share, gain2_share, bias2_share = (
        lax.psum_scatter(qkv_grad, "dp", scatter_dimension=0, tiled=True),
        lax.psum_scatter(out_grad, "dp", scatter_dimension=1, tiled=True),
        lax.psum_scatter(fc_grad, "dp", scatter_dimension=0, tiled=True),
        lax.psum_scatter(proj_grad, "dp", scatter_dimension=1, tiled=True),
        lax.psum_scatter(gain1_part, "dp", scatter_dimension=0, tiled=True),
        lax.psum_scatter(bias1_part, "dp", scatter_dimension=0, tiled=True),
        lax.psum_scatter(gain2_part, "dp", scatter_dimension=0, tiled=True),
        lax.psum_scatter(bias2_part, "dp", scatter_dimension=0, tiled=True),
    )
    gain1_sum, bias1_sum, gain2_sum, bias2_sum = lax.psum(
        (gain1_share, bias1_share, gain2_share, bias2_share), "tensor"
    )
    return (
        block_out,
        input_grad,
        qkv_sum,
        out_sum,
        fc_sum,
        proj_sum,
        gain1_sum,
        bias1_sum,
        gain2_sum,
        bias2_sum,
    )


def solution(mesh):
    placed = (
        P(("dp", "tensor"), None),
        P(("dp", "tensor"), None),
        P("dp", None),
        P("dp", None, "tensor"),
        P("tensor", "dp"),
        P("dp", "tensor"),
        P("tensor", "dp"),
        P("dp"),
        P("dp"),
        P("dp"),
        P("dp"),
    )
    return jax.shard_map(
        on_device,
        mesh=mesh,
        in_specs=placed,
        out_specs=(
            P(("dp", "tensor"), None),
            P(("dp", "tensor"), None),
            P("dp", None, "tensor"),
            P("tensor", "dp"),
            P("dp", "tensor"),
            P("tensor", "dp"),
            P("dp"),
            P("dp"),
            P("dp"),
            P("dp"),
        ),
        check_vma=False,
    )
```

profile of v0, /device:TPU:0, one launch (start us, length us, event | category | flops | bytes accessed | tf_op | source)
XLA Modules:
  0.0 1164.4 jit_solution(4583404668944278764)
XLA Ops:
  13.4 23.9 %all-reduce.10 = (bf16[768]{0:T(1024)(128)(2,1)}, bf16[768]{0:T(1024)(128)(2,1)}, bf16[768]{0:T(1024)(128)(2,1)S(1)}, bf16[768]{0:T(1024)(128)(2,1)S(1)}) all-reduce(bf16[768]{0:T(1024)(128)(2,1)S(1)} %dynamic-update-slice.3, bf16[768]{0:T(1024)(128)(2,1)S(1)} %dynamic-update-slice.2, ...), channel_id=1, replica_groups=mesh['dp'=8,'tensor'=4] {'dp'}, use_global_device_ids=true, to_apply=%add.3 | all-reduce | flops 3072 | bytes 12288
  43.6 35.5 %all_gather.39 = bf16[768,3,192]{2,1,0:T(4,128)(2,1)S(1)} all-gather(bf16[96,3,192]{2,1,0:T(4,128)(2,1)S(1)} %copy.32), channel_id=1, replica_groups=mesh['dp'=8,'tensor'=4] {'dp'}, dimensions={0}, use_global_device_ids=true | all-gather | bytes 995328 | tf_op jit(solution)/shard_map/all_gather | solution.py:132
  80.1 33.6 %all_gather.40 = bf16[192,768]{0,1:T(8,128)(2,1)} all-gather(bf16[192,96]{0,1:T(8,128)(2,1)S(1)} %copy.35), channel_id=1, replica_groups=mesh['dp'=8,'tensor'=4] {'dp'}, dimensions={1}, use_global_device_ids=true | all-gather | bytes 331776 | tf_op jit(solution)/shard_map/all_gather | solution.py:133
  119.7 122.1 %while.29 = (s32[]{:T(128)}, bf16[5,512,3,64]{1,3,2,0:T(8,128)(2,1)S(1)}, f32[5,3,512]{2,1,0:T(4,128)S(1)}, s32[5]{0:T(128)S(1)}, bf16[2560,3,64]{0,2,1:T(8,128)...) while((s32[]{:T(128)}, ...), condition=%wide.region_7.8_spmd.clone, body=%wide.region_4.7_spmd.clone.sunk | while | flops 1086686208 | bytes 54895824 | solution.py:75
  128.0 5.5 fusion.126
  133.5 10.6 fusion.127
  157.8 10.6 fusion.127
  182.2 10.6 fusion.127
  206.6 10.6 fusion.127
  231.0 10.6 fusion.127
  248.8 40.7 %reduce-scatter.11.cloned.1.call-done = bf16[640,768]{1,0:T(8,128)(2,1)} async-done(((bf16[2560,768]{1,0:T(8,128)(2,1)}), bf16[640,768]{1,0:T(8,128)(2,1)}) %reduce-scatter.11.cloned.1.call-update) | async-done | bytes 983056 | tf_op jit(solution)/shard_map/reduce_scatter | solution.py:161
  294.4 28.8 %all-gather.15.cloned.1.call-done = bf16[2560,768]{1,0:T(8,128)(2,1)} async-done(((bf16[640,768]{1,0:T(8,128)(2,1)}), bf16[2560,768]{1,0:T(8,128)(2,1)}) %all-gather.15.cloned.1.call-update) | async-done | bytes 3932176 | tf_op jit(solution)/shard_map/all_gather | solution.py:181
  323.2 8.8 fusion.75
  332.1 34.7 %all-gather.11.cloned.1.call-done = bf16[768,768]{1,0:T(8,128)(2,1)} async-done(((bf16[96,768]{1,0:T(8,128)(2,1)}), bf16[768,768]{1,0:T(8,128)(2,1)}) %all-gather.11.cloned.1.call-update) | async-done | bytes 1179664 | tf_op jit(solution)/shard_map/all_gather | solution.py:134
  366.7 33.4 %all-gather.9.cloned.1.call-done = bf16[2560,768]{1,0:T(8,128)(2,1)} async-done(((bf16[640,768]{1,0:T(8,128)(2,1)}), bf16[2560,768]{1,0:T(8,128)(2,1)}) %all-gather.9.cloned.1.call-update) | async-done | bytes 3932176 | tf_op jit(solution)/shard_map/all_gather | solution.py:169
  400.1 13.6 %fusion.43 = (bf16[2560,768]{1,0:T(8,128)(2,1)S(1)}, f32[2560,768]{1,0:T(8,128)}) fusion(f32[2560,768]{1,0:T(8,128)} %fusion.75, bf16[2560,768]{1,0:T(8,128)(2,1)} %all-gather.9.cloned.1.call-done, bf16[768,768]{1,0:T(8,128)(2,1)} %all-gather.11.cloned.1.call-done), kind=kOutput, calls=%fused_computation.55 | convolution fusion | flops 3059220480 | bytes 24772608 | tf_op jit(solution)/shard_map/dot_general | solution.py:170
  421.0 42.6 %reduce-scatter.15.cloned.1.call-done = bf16[640,768]{1,0:T(8,128)(2,1)} async-done(((bf16[2560,768]{1,0:T(8,128)(2,1)}), bf16[640,768]{1,0:T(8,128)(2,1)}) %reduce-scatter.15.cloned.1.call-update) | async-done | bytes 983056 | tf_op jit(solution)/shard_map/reduce_scatter | solution.py:187
  470.5 32.9 %all-gather.17.cloned.1.call-done = bf16[2560,768]{1,0:T(8,128)(2,1)} async-done(((bf16[640,768]{1,0:T(8,128)(2,1)}), bf16[2560,768]{1,0:T(8,128)(2,1)}) %all-gather.17.cloned.1.call-update) | async-done | bytes 3932176 | tf_op jit(solution)/shard_map/all_gather | solution.py:194
  512.9 323.7 %while.30 = (s32[]{:T(128)}, f32[2560,3,64]{0,2,1:T(8,128)}, f32[2560,3,64]{0,2,1:T(8,128)}, bf16[5,512,3,64]{1,0,3,2:T(8,128)(2,1)}, s32[5]{0:T(128)S(1)}, /*in...) while((s32[]{:T(128)}, f32[2560,3,64]{0,2,1:T(8,128)}, ...), condition=%wide.region_17.18_spmd.clone.clone, body=%wide.region_15.17_spmd.clone.clone.sunk | while | flops 2622784512 | bytes 218457456 | solution.py:117
  519.5 12.2 %fusion.139 = f32[2560,3,64]{0,2,1:T(8,128)} fusion(f32[3,512,2560]{2,1,0:T(8,128)S(1)} %fusion.137, f32[3,512]{1,0:T(4,128)S(1)} %dynamic-slice_bitcast_fusion.2, pred[512,2560]{1,0:T(8,128)(4,1)S(1)} %or_and_fusion.5, f32[2560,3,64]{0,2,1:T(8,128)} %get-tuple-element.492, pred[]{:T(512)S(6)} %compare.3, ...), kind=kOutput, calls=%fused_computation.30.clone.1 | convolution fusion | flops 531824640 | bytes 21174276 | tf_op jit(solution)/shard_map/while/body/eval_jaxpr/hqk,qhd->khd/dot_general | solution.py:98
  531.7 15.0 %multiply_reduce_fusion.3 = (f32[3,512]{1,0:T(4,128)S(1)}, f32[3,512,2560]{2,1,0:T(8,128)}) fusion(f32[3,512,2560]{2,1,0:T(8,128)S(1)} %fusion.137, f32[3,512]{1,0:T(4,128)S(1)} %dynamic-slice_bitcast_fusion.2, pred[512,2560]{1,0:T(8,128)(4,1)S(1)} %or_and_fusion.5, bf16[2560,3,64]{0,2,1:T(8,128)(2,1)S(1)} %copy-done.12, ...), kind=kOutput, calls=%fused_computation.19.clone.1 | convolution fusion | flops 534772224 | bytes 33959940 | tf_op jit(solution)/shard_map/while/body/eval_jaxpr/qhd,khd->hqk/dot_general | solution.py:101
  546.7 15.2 %subtract_convert_fusion.2 = bf16[3,512,2560]{2,1,0:T(8,128)(2,1)S(1)} fusion(f32[3,512,2560]{2,1,0:T(8,128)} %get-tuple-element.433, f32[3,512,2560]{2,1,0:T(8,128)} %copy-done, f32[3,512]{1,0:T(4,128)S(1)} %get-tuple-element.434, f32[3,512]{1,0:T(4,128)S(1)} %dynamic-slice_bitcast_fusion.2, pred[512,2560]{1,0:T(8,128)(4,1)S(1)} %or_and_fusion.5), kind=kLoop, calls=%fused_computation.18.clone.1 | loop fusion | flops 39321600 | bytes 40644608 | tf_op jit(solution)/shard_map/while/body/eval_jaxpr/convert_element_type | solution.py:105
  567.3 8.7 dynamic_update_slice.23
  582.4 14.4 %fusion.139 = f32[2560,3,64]{0,2,1:T(8,128)} fusion(f32[3,512,2560]{2,1,0:T(8,128)S(1)} %fusion.137, f32[3,512]{1,0:T(4,128)S(1)} %dynamic-slice_bitcast_fusion.2, pred[512,2560]{1,0:T(8,128)(4,1)S(1)} %or_and_fusion.5, f32[2560,3,64]{0,2,1:T(8,128)} %get-tuple-element.492, pred[]{:T(512)S(6)} %compare.3, ...), kind=kOutput, calls=%fused_computation.30.clone.1 | convolution fusion | flops 531824640 | bytes 21174276 | tf_op jit(solution)/shard_map/while/body/eval_jaxpr/hqk,qhd->khd/dot_general | solution.py:98
  596.8 15.0 %multiply_reduce_fusion.3 = (f32[3,512]{1,0:T(4,128)S(1)}, f32[3,512,2560]{2,1,0:T(8,128)}) fusion(f32[3,512,2560]{2,1,0:T(8,128)S(1)} %fusion.137, f32[3,512]{1,0:T(4,128)S(1)} %dynamic-slice_bitcast_fusion.2, pred[512,2560]{1,0:T(8,128)(4,1)S(1)} %or_and_fusion.5, bf16[2560,3,64]{0,2,1:T(8,128)(2,1)S(1)} %copy-done.12, ...), kind=kOutput, calls=%fused_computation.19.clone.1 | convolution fusion | flops 534772224 | bytes 33959940 | tf_op jit(solution)/shard_map/while/body/eval_jaxpr/qhd,khd->hqk/dot_general | solution.py:101
  611.8 15.2 %subtract_convert_fusion.2 = bf16[3,512,2560]{2,1,0:T(8,128)(2,1)S(1)} fusion(f32[3,512,2560]{2,1,0:T(8,128)} %get-tuple-element.433, f32[3,512,2560]{2,1,0:T(8,128)} %copy-done, f32[3,512]{1,0:T(4,128)S(1)} %get-tuple-element.434, f32[3,512]{1,0:T(4,128)S(1)} %dynamic-slice_bitcast_fusion.2, pred[512,2560]{1,0:T(8,128)(4,1)S(1)} %or_and_fusion.5), kind=kLoop, calls=%fused_computation.18.clone.1 | loop fusion | flops 39321600 | bytes 40644608 | tf_op jit(solution)/shard_map/while/body/eval_jaxpr/convert_element_type | solution.py:105
  632.3 8.7 dynamic_update_slice.23
  647.4 14.4 %fusion.139 = f32[2560,3,64]{0,2,1:T(8,128)} fusion(f32[3,512,2560]{2,1,0:T(8,128)S(1)} %fusion.137, f32[3,512]{1,0:T(4,128)S(1)} %dynamic-slice_bitcast_fusion.2, pred[512,2560]{1,0:T(8,128)(4,1)S(1)} %or_and_fusion.5, f32[2560,3,64]{0,2,1:T(8,128)} %get-tuple-element.492, pred[]{:T(512)S(6)} %compare.3, ...), kind=kOutput, calls=%fused_computation.30.clone.1 | convolution fusion | flops 531824640 | bytes 21174276 | tf_op jit(solution)/shard_map/while/body/eval_jaxpr/hqk,qhd->khd/dot_general | solution.py:98
  661.8 15.0 %multiply_reduce_fusion.3 = (f32[3,512]{1,0:T(4,128)S(1)}, f32[3,512,2560]{2,1,0:T(8,128)}) fusion(f32[3,512,2560]{2,1,0:T(8,128)S(1)} %fusion.137, f32[3,512]{1,0:T(4,128)S(1)} %dynamic-slice_bitcast_fusion.2, pred[512,2560]{1,0:T(8,128)(4,1)S(1)} %or_and_fusion.5, bf16[2560,3,64]{0,2,1:T(8,128)(2,1)S(1)} %copy-done.12, ...), kind=kOutput, calls=%fused_computation.19.clone.1 | convolution fusion | flops 534772224 | bytes 33959940 | tf_op jit(solution)/shard_map/while/body/eval_jaxpr/qhd,khd->hqk/dot_general | solution.py:101
  676.8 15.2 %subtract_convert_fusion.2 = bf16[3,512,2560]{2,1,0:T(8,128)(2,1)S(1)} fusion(f32[3,512,2560]{2,1,0:T(8,128)} %get-tuple-element.433, f32[3,512,2560]{2,1,0:T(8,128)} %copy-done, f32[3,512]{1,0:T(4,128)S(1)} %get-tuple-element.434, f32[3,512]{1,0:T(4,128)S(1)} %dynamic-slice_bitcast_fusion.2, pred[512,2560]{1,0:T(8,128)(4,1)S(1)} %or_and_fusion.5), kind=kLoop, calls=%fused_computation.18.clone.1 | loop fusion | flops 39321600 | bytes 40644608 | tf_op jit(solution)/shard_map/while/body/eval_jaxpr/convert_element_type | solution.py:105
  697.4 8.7 dynamic_update_slice.23
  712.5 14.4 %fusion.139 = f32[2560,3,64]{0,2,1:T(8,128)} fusion(f32[3,512,2560]{2,1,0:T(8,128)S(1)} %fusion.137, f32[3,512]{1,0:T(4,128)S(1)} %dynamic-slice_bitcast_fusion.2, pred[512,2560]{1,0:T(8,128)(4,1)S(1)} %or_and_fusion.5, f32[2560,3,64]{0,2,1:T(8,128)} %get-tuple-element.492, pred[]{:T(512)S(6)} %compare.3, ...), kind=kOutput, calls=%fused_computation.30.clone.1 | convolution fusion | flops 531824640 | bytes 21174276 | tf_op jit(solution)/shard_map/while/body/eval_jaxpr/hqk,qhd->khd/dot_general | solution.py:98
  726.9 15.0 %multiply_reduce_fusion.3 = (f32[3,512]{1,0:T(4,128)S(1)}, f32[3,512,2560]{2,1,0:T(8,128)}) fusion(f32[3,512,2560]{2,1,0:T(8,128)S(1)} %fusion.137, f32[3,512]{1,0:T(4,128)S(1)} %dynamic-slice_bitcast_fusion.2, pred[512,2560]{1,0:T(8,128)(4,1)S(1)} %or_and_fusion.5, bf16[2560,3,64]{0,2,1:T(8,128)(2,1)S(1)} %copy-done.12, ...), kind=kOutput, calls=%fused_computation.19.clone.1 | convolution fusion | flops 534772224 | bytes 33959940 | tf_op jit(solution)/shard_map/while/body/eval_jaxpr/qhd,khd->hqk/dot_general | solution.py:101
  741.9 15.2 %subtract_convert_fusion.2 = bf16[3,512,2560]{2,1,0:T(8,128)(2,1)S(1)} fusion(f32[3,512,2560]{2,1,0:T(8,128)} %get-tuple-element.433, f32[3,512,2560]{2,1,0:T(8,128)} %copy-done, f32[3,512]{1,0:T(4,128)S(1)} %get-tuple-element.434, f32[3,512]{1,0:T(4,128)S(1)} %dynamic-slice_bitcast_fusion.2, pred[512,2560]{1,0:T(8,128)(4,1)S(1)} %or_and_fusion.5), kind=kLoop, calls=%fused_computation.18.clone.1 | loop fusion | flops 39321600 | bytes 40644608 | tf_op jit(solution)/shard_map/while/body/eval_jaxpr/convert_element_type | solution.py:105
  762.5 8.7 dynamic_update_slice.23
  777.6 14.4 %fusion.139 = f32[2560,3,64]{0,2,1:T(8,128)} fusion(f32[3,512,2560]{2,1,0:T(8,128)S(1)} %fusion.137, f32[3,512]{1,0:T(4,128)S(1)} %dynamic-slice_bitcast_fusion.2, pred[512,2560]{1,0:T(8,128)(4,1)S(1)} %or_and_fusion.5, f32[2560,3,64]{0,2,1:T(8,128)} %get-tuple-element.492, pred[]{:T(512)S(6)} %compare.3, ...), kind=kOutput, calls=%fused_computation.30.clone.1 | convolution fusion | flops 531824640 | bytes 21174276 | tf_op jit(solution)/shard_map/while/body/eval_jaxpr/hqk,qhd->khd/dot_general | solution.py:98
  792.0 15.0 %multiply_reduce_fusion.3 = (f32[3,512]{1,0:T(4,128)S(1)}, f32[3,512,2560]{2,1,0:T(8,128)}) fusion(f32[3,512,2560]{2,1,0:T(8,128)S(1)} %fusion.137, f32[3,512]{1,0:T(4,128)S(1)} %dynamic-slice_bitcast_fusion.2, pred[512,2560]{1,0:T(8,128)(4,1)S(1)} %or_and_fusion.5, bf16[2560,3,64]{0,2,1:T(8,128)(2,1)S(1)} %copy-done.12, ...), kind=kOutput, calls=%fused_computation.19.clone.1 | convolution fusion | flops 534772224 | bytes 33959940 | tf_op jit(solution)/shard_map/while/body/eval_jaxpr/qhd,khd->hqk/dot_general | solution.py:101
  807.0 15.2 %subtract_convert_fusion.2 = bf16[3,512,2560]{2,1,0:T(8,128)(2,1)S(1)} fusion(f32[3,512,2560]{2,1,0:T(8,128)} %get-tuple-element.433, f32[3,512,2560]{2,1,0:T(8,128)} %copy-done, f32[3,512]{1,0:T(4,128)S(1)} %get-tuple-element.434, f32[3,512]{1,0:T(4,128)S(1)} %dynamic-slice_bitcast_fusion.2, pred[512,2560]{1,0:T(8,128)(4,1)S(1)} %or_and_fusion.5), kind=kLoop, calls=%fused_computation.18.clone.1 | loop fusion | flops 39321600 | bytes 40644608 | tf_op jit(solution)/shard_map/while/body/eval_jaxpr/convert_element_type | solution.py:105
  827.5 8.7 dynamic_update_slice.23
  849.9 9.9 convolution_convert_fusion.1
  859.9 8.1 fusion.76
  868.2 9.6 fusion.73
  877.9 7.7 fusion.44
  893.8 37.1 %all-reduce.8 = (f32[768]{0:T(1024)S(1)}, f32[768]{0:T(1024)S(1)}, f32[768]{0:T(1024)S(1)}, f32[768]{0:T(1024)S(1)}) all-reduce(f32[768]{0:T(1024)S(1)} %get-tuple-element.224, f32[768]{0:T(1024)S(1)} %get-tuple-element.229, f32[768]{0:T(1024)S(1)} %copy-done.34, ...), channel_id=10, replica_groups=mesh['dp'=8,'tensor'=4] {'dp'}, use_global_device_ids=true, to_apply=%region_26.27.clone | all-reduce | flops 3072 | bytes 24576
  931.2 6.4 all-reduce.9
  941.8 68.8 %reduce-scatter.21.cloned.1.call-done = f32[96,768]{1,0:T(8,128)} async-done(((f32[768,768]{1,0:T(8,128)}), f32[96,768]{1,0:T(8,128)}) %reduce-scatter.21.cloned.1.call-update) | async-done | bytes 294928 | tf_op jit(solution)/shard_map/reduce_scatter | solution.py:216
  1010.6 73.1 %reduce-scatter.23.cloned.1.call-done = f32[768,96]{0,1:T(8,128)} async-done(((f32[768,768]{0,1:T(8,128)}), f32[768,96]{0,1:T(8,128)}) %reduce-scatter.23.cloned.1.call-update) | async-done | bytes 294928 | tf_op jit(solution)/shard_map/reduce_scatter | solution.py:217
  1083.8 73.1 %reduce-scatter.19.cloned.1.call-done = f32[96,3,192]{2,0,1:T(8,128)} async-done(((f32[768,3,192]{2,0,1:T(8,128)}), f32[96,3,192]{2,0,1:T(8,128)}) %reduce-scatter.19.cloned.1.call-update) | async-done | bytes 221200 | tf_op jit(solution)/shard_map/reduce_scatter | solution.py:214
  (300 shorter events, 193.6 us)
Async XLA Ops:
  8.0 35.1 %copy-start.40 = (s32[1,8]{1,0:T(1,128)S(1)}, s32[1,8]{1,0:T(1,128)}, u32[]{:S(2)}) copy-start(s32[1,8]{1,0:T(1,128)} %param.17) | copy-start | bytes 100
  8.0 35.3 %copy-start.29 = (bf16[192,96]{1,0:T(8,128)(2,1)S(1)}, bf16[192,96]{1,0:T(8,128)(2,1)}, u32[]{:S(2)}) copy-start(bf16[192,96]{1,0:T(8,128)(2,1)} %param.19) | copy-start | bytes 110596
  8.0 35.4 %copy-start.16 = (bf16[96,3,192]{2,0,1:T(8,128)(2,1)S(1)}, bf16[96,3,192]{2,0,1:T(8,128)(2,1)}, u32[]{:S(2)}) copy-start(bf16[96,3,192]{2,0,1:T(8,128)(2,1)} %param.18) | copy-start | bytes 331780
  8.0 105.7 %all-gather.7.cloned.1.call-start = ((), (), s32[]{:S(2)}) async-start(), calls=%async_computation.8 | async-start | bytes 4915200 | tf_op jit(solution)/shard_map/all_gather | solution.py:153
  43.0 246.5 %reduce-scatter.11.cloned.1.call-start = ((), (), s32[]{:S(2)}) async-start(), calls=%async_computation.9 | async-start | bytes 4915200 | tf_op jit(solution)/shard_map/reduce_scatter | solution.py:161
  80.0 38.3 %copy-start.14 = (bf16[768,3,192]{0,2,1:T(8,128)(2,1)}, bf16[768,3,192]{0,2,1:T(8,128)(2,1)S(1)}, u32[]{:S(2)}) copy-start(bf16[768,3,192]{0,2,1:T(8,128)(2,1)S(1)} %copy.33) | copy-start | bytes 2654212
  246.9 42.6 %copy-start.1 = (bf16[640,768]{1,0:T(8,128)(2,1)S(1)}, bf16[640,768]{1,0:T(8,128)(2,1)}, u32[]{:S(2)}) copy-start(bf16[640,768]{1,0:T(8,128)(2,1)} %param.15) | copy-start | bytes 2949124
  247.0 47.5 %all-gather.13.cloned.1.call-start = ((), (), s32[]{:S(2)}) async-start(), calls=%async_computation.12 | async-start | bytes 1327104 | tf_op jit(solution)/shard_map/all_gather | solution.py:135
  247.5 75.7 %all-gather.15.cloned.1.call-start = ((), (), s32[]{:S(2)}) async-start(), calls=%async_computation.14 | async-start | bytes 4915200 | tf_op jit(solution)/shard_map/all_gather | solution.py:181
  248.1 118.6 %all-gather.11.cloned.1.call-start = ((), (), s32[]{:S(2)}) async-start(), calls=%async_computation.11 | async-start | bytes 1327104 | tf_op jit(solution)/shard_map/all_gather | solution.py:134
  248.7 151.4 %all-gather.9.cloned.1.call-start = ((), (), s32[]{:S(2)}) async-start(), calls=%async_computation.10 | async-start | bytes 4915200 | tf_op jit(solution)/shard_map/all_gather | solution.py:169
  248.8 217.6 %copy-start.21 = (f32[768]{0:T(1024)}, f32[768]{0:T(1024)S(1)}, u32[]{:S(2)}) copy-start(f32[768]{0:T(1024)S(1)} %convert_element_type.109) | copy-start | bytes 9220
  291.2 175.2 %copy-start.17 = (f32[640]{0:T(1024)}, f32[640]{0:T(1024)S(1)}, u32[]{:S(2)}) copy-start(f32[640]{0:T(1024)S(1)} %broadcast_multiply_fusion.4) | copy-start | bytes 7684
  292.9 173.5 %copy-start.23 = (f32[640]{0:T(1024)}, f32[640]{0:T(1024)S(1)}, u32[]{:S(2)}) copy-start(f32[640]{0:T(1024)S(1)} %add_rsqrt_fusion) | copy-start | bytes 7684
  294.4 169.2 %reduce-scatter.15.cloned.1.call-start = ((), (), s32[]{:S(2)}) async-start(), calls=%async_computation.15 | async-start | bytes 4915200 | tf_op jit(solution)/shard_map/reduce_scatter | solution.py:187
  400.1 15.6 %copy-start.39 = (bf16[768,768]{1,0:T(8,128)(2,1)S(1)}, bf16[768,768]{1,0:T(8,128)(2,1)}, u32[]{:S(2)}) copy-start(bf16[768,768]{1,0:T(8,128)(2,1)} %all-gather.11.cloned.1.call-done) | copy-start | bytes 3538948
  420.5 82.9 %all-gather.17.cloned.1.call-start = ((), (), s32[]{:S(2)}) async-start(), calls=%async_computation.16 | async-start | bytes 4915200 | tf_op jit(solution)/shard_map/all_gather | solution.py:194
  470.4 416.2 %reduce-scatter.25.cloned.1.call-start = ((), (), s32[]{:S(2)}) async-start(), calls=%async_computation.21 | async-start | bytes 884736
  508.3 383.3 %reduce-scatter.17.cloned.1.call-start = ((), (), s32[]{:S(2)}) async-start(), calls=%async_computation.17 | async-start | bytes 4915200 | tf_op jit(solution)/shard_map/reduce_scatter | solution.py:207
  519.5 12.2 %copy-start = (f32[3,512,2560]{2,1,0:T(8,128)}, f32[3,512,2560]{2,1,0:T(8,128)S(1)}, u32[]{:S(2)}) copy-start(f32[3,512,2560]{2,1,0:T(8,128)S(1)} %fusion.137) | copy-start | bytes 47185924 | tf_op jit(solution)/shard_map/while
  519.5 12.2 %copy-start.12 = (bf16[2560,3,64]{0,2,1:T(8,128)(2,1)S(1)}, bf16[2560,3,64]{0,2,1:T(8,128)(2,1)}, u32[]{:S(2)}) copy-start(bf16[2560,3,64]{0,2,1:T(8,128)(2,1)} %get-tuple-element.517) | copy-start | bytes 2949124 | tf_op jit(solution)/shard_map/while
  567.0 9.0 copy-start.4
  582.4 14.4 %copy-start = (f32[3,512,2560]{2,1,0:T(8,128)}, f32[3,512,2560]{2,1,0:T(8,128)S(1)}, u32[]{:S(2)}) copy-start(f32[3,512,2560]{2,1,0:T(8,128)S(1)} %fusion.137) | copy-start | bytes 47185924 | tf_op jit(solution)/shard_map/while
  582.4 14.4 %copy-start.12 = (bf16[2560,3,64]{0,2,1:T(8,128)(2,1)S(1)}, bf16[2560,3,64]{0,2,1:T(8,128)(2,1)}, u32[]{:S(2)}) copy-start(bf16[2560,3,64]{0,2,1:T(8,128)(2,1)} %get-tuple-element.517) | copy-start | bytes 2949124 | tf_op jit(solution)/shard_map/while
  632.0 9.0 copy-start.4
  647.4 14.4 %copy-start = (f32[3,512,2560]{2,1,0:T(8,128)}, f32[3,512,2560]{2,1,0:T(8,128)S(1)}, u32[]{:S(2)}) copy-start(f32[3,512,2560]{2,1,0:T(8,128)S(1)} %fusion.137) | copy-start | bytes 47185924 | tf_op jit(solution)/shard_map/while
  647.4 14.4 %copy-start.12 = (bf16[2560,3,64]{0,2,1:T(8,128)(2,1)S(1)}, bf16[2560,3,64]{0,2,1:T(8,128)(2,1)}, u32[]{:S(2)}) copy-start(bf16[2560,3,64]{0,2,1:T(8,128)(2,1)} %get-tuple-element.517) | copy-start | bytes 2949124 | tf_op jit(solution)/shard_map/while
  697.1 9.0 copy-start.4
  712.5 14.4 %copy-start = (f32[3,512,2560]{2,1,0:T(8,128)}, f32[3,512,2560]{2,1,0:T(8,128)S(1)}, u32[]{:S(2)}) copy-start(f32[3,512,2560]{2,1,0:T(8,128)S(1)} %fusion.137) | copy-start | bytes 47185924 | tf_op jit(solution)/shard_map/while
  712.5 14.4 %copy-start.12 = (bf16[2560,3,64]{0,2,1:T(8,128)(2,1)S(1)}, bf16[2560,3,64]{0,2,1:T(8,128)(2,1)}, u32[]{:S(2)}) copy-start(bf16[2560,3,64]{0,2,1:T(8,128)(2,1)} %get-tuple-element.517) | copy-start | bytes 2949124 | tf_op jit(solution)/shard_map/while
  762.2 9.0 copy-start.4
  777.6 14.4 %copy-start = (f32[3,512,2560]{2,1,0:T(8,128)}, f32[3,512,2560]{2,1,0:T(8,128)S(1)}, u32[]{:S(2)}) copy-start(f32[3,512,2560]{2,1,0:T(8,128)S(1)} %fusion.137) | copy-start | bytes 47185924 | tf_op jit(solution)/shard_map/while
  777.6 14.4 %copy-start.12 = (bf16[2560,3,64]{0,2,1:T(8,128)(2,1)S(1)}, bf16[2560,3,64]{0,2,1:T(8,128)(2,1)}, u32[]{:S(2)}) copy-start(bf16[2560,3,64]{0,2,1:T(8,128)(2,1)} %get-tuple-element.517) | copy-start | bytes 2949124 | tf_op jit(solution)/shard_map/while
  848.7 88.9 %reduce-scatter.13.cloned.1.call-start = ((), (), s32[]{:S(2)}) async-start(), calls=%async_computation.13 | async-start | bytes 4915200 | tf_op jit(solution)/shard_map/reduce_scatter | solution.py:174
  859.8 150.8 %reduce-scatter.21.cloned.1.call-start = ((), (), s32[]{:S(2)}) async-start(), calls=%async_computation.19 | async-start | bytes 2654208 | tf_op jit(solution)/shard_map/reduce_scatter | solution.py:216
  868.0 215.8 %reduce-scatter.23.cloned.1.call-start = ((), (), s32[]{:S(2)}) async-start(), calls=%async_computation.20 | async-start | bytes 2654208 | tf_op jit(solution)/shard_map/reduce_scatter | solution.py:217
  877.8 279.1 %reduce-scatter.19.cloned.1.call-start = ((), (), s32[]{:S(2)}) async-start(), calls=%async_computation.18 | async-start | bytes 2654208 | tf_op jit(solution)/shard_map/reduce_scatter | solution.py:214
  877.9 13.7 %copy-start.2 = (bf16[640,768]{1,0:T(8,128)(2,1)S(1)}, bf16[640,768]{1,0:T(8,128)(2,1)}, u32[]{:S(2)}) copy-start(bf16[640,768]{1,0:T(8,128)(2,1)} %param.15) | copy-start | bytes 2949124
  877.9 13.7 %copy-start.20 = (f32[640]{0:T(1024)S(1)}, f32[640]{0:T(1024)}, u32[]{:S(2)}) copy-start(f32[640]{0:T(1024)} %copy-done.19) | copy-start | bytes 7684
  877.9 13.7 %copy-start.26 = (f32[768]{0:T(1024)S(1)}, f32[768]{0:T(1024)}, u32[]{:S(2)}) copy-start(f32[768]{0:T(1024)} %copy-done.25) | copy-start | bytes 9220
  877.9 13.7 %copy-start.28 = (f32[640]{0:T(1024)S(1)}, f32[640]{0:T(1024)}, u32[]{:S(2)}) copy-start(f32[640]{0:T(1024)} %copy-done.27) | copy-start | bytes 7684
  885.7 51.9 %copy-start.6 = (bf16[640,768]{1,0:T(8,128)(2,1)S(1)}, bf16[640,768]{1,0:T(8,128)(2,1)}, u32[]{:S(2)}) copy-start(bf16[640,768]{1,0:T(8,128)(2,1)} %reduce-scatter.11.cloned.1.call-done) | copy-start | bytes 2949124
  885.7 51.9 %copy-start.7 = (bf16[640,768]{1,0:T(8,128)(2,1)S(1)}, bf16[640,768]{1,0:T(8,128)(2,1)}, u32[]{:S(2)}) copy-start(bf16[640,768]{1,0:T(8,128)(2,1)} %param.16) | copy-start | bytes 2949124
  885.7 51.9 %copy-start.18 = (f32[640]{0:T(1024)S(1)}, f32[640]{0:T(1024)}, u32[]{:S(2)}) copy-start(f32[640]{0:T(1024)} %copy-done.17) | copy-start | bytes 7684
  885.7 51.9 %copy-start.22 = (f32[768]{0:T(1024)S(1)}, f32[768]{0:T(1024)}, u32[]{:S(2)}) copy-start(f32[768]{0:T(1024)} %copy-done.21) | copy-start | bytes 9220
  885.7 51.9 %copy-start.24 = (f32[640]{0:T(1024)S(1)}, f32[640]{0:T(1024)}, u32[]{:S(2)}) copy-start(f32[640]{0:T(1024)} %copy-done.23) | copy-start | bytes 7684
  885.7 51.9 %copy-start.31 = (f32[640]{0:T(1024)S(1)}, f32[640]{0:T(1024)}, u32[]{:S(2)}) copy-start(f32[640]{0:T(1024)} %copy-done.30) | copy-start | bytes 7684
  885.7 51.9 %copy-start.33 = (f32[640]{0:T(1024)S(1)}, f32[640]{0:T(1024)}, u32[]{:S(2)}) copy-start(f32[640]{0:T(1024)} %copy-done.32) | copy-start | bytes 7684
  (24 other events, 73.9 us)
Sparse Core Ops, SparseCore 0:
  43.1 30.2 all-gather.6
  247.1 42.4 reduce-scatter.10
  420.6 42.8 reduce-scatter.14
Sparse Core Ops, SparseCore 1:
  249.6 40.9 all-gather.12
  292.0 31.2 all-gather.14
  325.3 41.4 all-gather.10
  368.9 31.2 all-gather.8
  470.5 32.8 all-gather.16
  508.4 63.3 reduce-scatter.24
  848.7 42.8 reduce-scatter.16
  894.0 42.8 reduce-scatter.12
  940.8 69.8 reduce-scatter.20
  1014.7 69.0 reduce-scatter.22
  1087.7 69.1 reduce-scatter.18
where the time goes:
time: 1170 us; the launch traced here: 1160 us
  waiting for transfers between devices  433 us (37%)
  matrix products  348 us (30%)
  other arithmetic  148 us (13%)
  blocking collectives  137 us (12%)
  local copies, waits for them, and re-layouts  71.7 us (6%)
  between operations  17.7 us (2%)
    convert_element_type x5, other arithmetic, step(): score_grad = (prob * weight_grad - signed * inner).astype(jnp.bfloat16)  76.2 us
    dot_general x5, matrix products, step(): jnp.einsum('qhd,khd->hqk', grad_block, values, preferred_element_type=jnp...  75 us
    reduce_scatter x1, waiting for transfers between devices, on_device(): lax.psum_scatter(qkv_grad, 'dp', scatter_dimension=0, tiled=True)  73.1 us
    reduce_scatter x1, waiting for transfers between devices, on_device(): lax.psum_scatter(proj_grad, 'dp', scatter_dimension=1, tiled=True)  73.1 us
    dot_general x5, matrix products, step(): jnp.einsum('hqk,qhd->khd', rounded, grad_block, preferred_element_type=jn...  69.8 us
    reduce_scatter x1, waiting for transfers between devices, on_device(): lax.psum_scatter(fc_grad, 'dp', scatter_dimension=0, tiled=True)  68.8 us
    unnamed x2, blocking collectives  61 us
    dot_general x5, matrix products, one(): jnp.einsum('hqk,khd->qhd', weights, values, preferred_element_type=jnp.fl...  52.9 us
  transfers between devices with their start and end apart: 14, of which 10 were waited for; matrix products, arithmetic and copies ran while one was open for 34% of the time, Pallas kernels for 0%

commit v1 on v0

--- a/solution.py
+++ b/solution.py
@@ -166,7 +166,9 @@
     ).astype(jnp.float32)
     normed2, factor2 = normalize(resid)
     lowered2 = (normed2 * gain2 + bias2).astype(jnp.bfloat16)
-    all_norm2 = lax.all_gather(lowered2, "tensor", axis=0, tiled=True)
+    all_norm2 = jnp.concatenate(
+        lax.all_to_all(jnp.stack([lowered2] * lax.axis_size("tensor")), "tensor", 0, 0), axis=0
+    )
     hidden_pre = jnp.dot(all_norm2, fc_full, preferred_element_type=jnp.float32)
     hidden, gelu_pull = jax.vjp(gelu_tanh, hidden_pre)
     hidden_low = hidden.astype(jnp.bfloat16)

time: 1170 us -> 1150 us (0.983)
  waiting for transfers between devices: 433 us -> 411 us
    all_gather x1 -> x0, waiting for transfers between devices: 33.4 us -> none  [on_device(): all_norm2 = lax.all_gather(lowered2, 'tensor', axis=0, tiled=True)]
  transfers between devices with their start and end apart: 14 -> 14, of which waited for: 10 -> 9; matrix products, arithmetic and copies ran while one was open for 34% -> 34% of each run, Pallas kernels for 0% -> 0%
where the time goes in v1:
time: 1150 us
  waiting for transfers between devices  411 us (36%)
  matrix products  349 us (30%)
  other arithmetic  147 us (13%)
  blocking collectives  136 us (12%)
  local copies, waits for them, and re-layouts  73.6 us (6%)
  between operations  17.6 us (2%)
    convert_element_type x5, other arithmetic, step(): score_grad = (prob * weight_grad - signed * inner).astype(jnp.bfloat16)  76.2 us
    dot_general x5, matrix products, step(): jnp.einsum('qhd,khd->hqk', grad_block, values, preferred_element_type=jnp...  75.1 us
    reduce_scatter x1, waiting for transfers between devices, on_device(): lax.psum_scatter(qkv_grad, 'dp', scatter_dimension=0, tiled=True)  73.3 us
    reduce_scatter x1, waiting for transfers between devices, on_device(): lax.psum_scatter(proj_grad, 'dp', scatter_dimension=1, tiled=True)  72.9 us
    dot_general x5, matrix products, step(): jnp.einsum('hqk,qhd->khd', rounded, grad_block, preferred_element_type=jn...  69.8 us
    reduce_scatter x1, waiting for transfers between devices, on_device(): lax.psum_scatter(fc_grad, 'dp', scatter_dimension=0, tiled=True)  69.1 us
    unnamed x2, blocking collectives  61 us
    dot_general x5, matrix products, one(): jnp.einsum('hqk,khd->qhd', weights, values, preferred_element_type=jnp.fl...  52.9 us
  transfers between devices with their start and end apart: 14, of which 9 were waited for; matrix products, arithmetic and copies ran while one was open for 34% of the time, Pallas kernels for 0%

profile of v1, /device:TPU:0, one launch (start us, length us, event | category | flops | bytes accessed | tf_op | source)
XLA Modules:
  0.0 1148.1 jit_solution(13983338065964707319)
XLA Ops:
  13.4 23.9 %all-reduce.10 = (bf16[768]{0:T(1024)(128)(2,1)}, bf16[768]{0:T(1024)(128)(2,1)}, bf16[768]{0:T(1024)(128)(2,1)S(1)}, bf16[768]{0:T(1024)(128)(2,1)S(1)}) all-reduce(bf16[768]{0:T(1024)(128)(2,1)S(1)} %dynamic-update-slice.3, bf16[768]{0:T(1024)(128)(2,1)S(1)} %dynamic-update-slice.2, ...), channel_id=1, replica_groups=mesh['dp'=8,'tensor'=4] {'dp'}, use_global_device_ids=true, to_apply=%add.3 | all-reduce | flops 3072 | bytes 12288
  43.6 35.5 %all_gather.36 = bf16[768,3,192]{2,1,0:T(4,128)(2,1)S(1)} all-gather(bf16[96,3,192]{2,1,0:T(4,128)(2,1)S(1)} %copy.32), channel_id=1, replica_groups=mesh['dp'=8,'tensor'=4] {'dp'}, dimensions={0}, use_global_device_ids=true | all-gather | bytes 995328 | tf_op jit(solution)/shard_map/all_gather | solution.py:132
  80.1 33.4 %all_gather.37 = bf16[192,768]{0,1:T(8,128)(2,1)} all-gather(bf16[192,96]{0,1:T(8,128)(2,1)S(1)} %copy.35), channel_id=1, replica_groups=mesh['dp'=8,'tensor'=4] {'dp'}, dimensions={1}, use_global_device_ids=true | all-gather | bytes 331776 | tf_op jit(solution)/shard_map/all_gather | solution.py:133
  119.5 122.4 %while.29 = (s32[]{:T(128)}, bf16[5,512,3,64]{1,3,2,0:T(8,128)(2,1)S(1)}, f32[5,3,512]{2,1,0:T(4,128)S(1)}, s32[5]{0:T(128)S(1)}, bf16[2560,3,64]{0,2,1:T(8,128)...) while((s32[]{:T(128)}, ...), condition=%wide.region_7.8_spmd.clone, body=%wide.region_4.7_spmd.clone.sunk | while | flops 1086686208 | bytes 54895824 | solution.py:75
  127.8 5.5 fusion.126
  133.3 10.6 fusion.127
  157.7 10.6 fusion.127
  182.1 10.6 fusion.127
  201.0 5.5 fusion.126
  206.4 10.6 fusion.127
  230.8 10.6 fusion.127
  248.4 41.4 %reduce-scatter.11.cloned.1.call-done = bf16[640,768]{1,0:T(8,128)(2,1)} async-done(((bf16[2560,768]{1,0:T(8,128)(2,1)}), bf16[640,768]{1,0:T(8,128)(2,1)}) %reduce-scatter.11.cloned.1.call-update) | async-done | bytes 983056 | tf_op jit(solution)/shard_map/reduce_scatter | solution.py:161
  301.3 40.3 %all-gather.12.cloned.1.call-done = bf16[2560,768]{1,0:T(8,128)(2,1)} async-done(((bf16[640,768]{1,0:T(8,128)(2,1)}), bf16[2560,768]{1,0:T(8,128)(2,1)}) %all-gather.12.cloned.1.call-update) | async-done | bytes 3932176 | tf_op jit(solution)/shard_map/all_gather | solution.py:183
  341.7 8.8 fusion.75
  350.5 34.7 %all-gather.8.cloned.1.call-done = bf16[768,768]{1,0:T(8,128)(2,1)} async-done(((bf16[96,768]{1,0:T(8,128)(2,1)}), bf16[768,768]{1,0:T(8,128)(2,1)}) %all-gather.8.cloned.1.call-update) | async-done | bytes 1179664 | tf_op jit(solution)/shard_map/all_gather | solution.py:134
  385.2 13.8 %fusion.43 = (bf16[2560,768]{1,0:T(8,128)(2,1)S(1)}, f32[2560,768]{1,0:T(8,128)}) fusion(f32[2560,768]{1,0:T(8,128)} %fusion.75, bf16[2560,768]{1,0:T(8,128)(2,1)} %bitcast.8, bf16[768,768]{1,0:T(8,128)(2,1)} %all-gather.8.cloned.1.call-done), kind=kOutput, calls=%fused_computation.55 | convolution fusion | flops 3059220480 | bytes 24772608 | tf_op jit(solution)/shard_map/dot_general | solution.py:172
  405.8 41.2 %reduce-scatter.15.cloned.1.call-done = bf16[640,768]{1,0:T(8,128)(2,1)} async-done(((bf16[2560,768]{1,0:T(8,128)(2,1)}), bf16[640,768]{1,0:T(8,128)(2,1)}) %reduce-scatter.15.cloned.1.call-update) | async-done | bytes 983056 | tf_op jit(solution)/shard_map/reduce_scatter | solution.py:189
  453.9 33.1 %all-gather.14.cloned.1.call-done = bf16[2560,768]{1,0:T(8,128)(2,1)} async-done(((bf16[640,768]{1,0:T(8,128)(2,1)}), bf16[2560,768]{1,0:T(8,128)(2,1)}) %all-gather.14.cloned.1.call-update) | async-done | bytes 3932176 | tf_op jit(solution)/shard_map/all_gather | solution.py:196
  496.5 323.7 %while.30 = (s32[]{:T(128)}, f32[2560,3,64]{0,2,1:T(8,128)}, f32[2560,3,64]{0,2,1:T(8,128)}, bf16[5,512,3,64]{1,0,3,2:T(8,128)(2,1)}, s32[5]{0:T(128)S(1)}, /*in...) while((s32[]{:T(128)}, f32[2560,3,64]{0,2,1:T(8,128)}, ...), condition=%wide.region_17.18_spmd.clone.clone, body=%wide.region_15.17_spmd.clone.clone.sunk | while | flops 2622784512 | bytes 218457456 | solution.py:117
  503.3 12.2 %fusion.139 = f32[2560,3,64]{0,2,1:T(8,128)} fusion(f32[3,512,2560]{2,1,0:T(8,128)S(1)} %fusion.137, f32[3,512]{1,0:T(4,128)S(1)} %dynamic-slice_bitcast_fusion.2, pred[512,2560]{1,0:T(8,128)(4,1)S(1)} %or_and_fusion.5, f32[2560,3,64]{0,2,1:T(8,128)} %get-tuple-element.492, pred[]{:T(512)S(6)} %compare.3, ...), kind=kOutput, calls=%fused_computation.30.clone.1 | convolution fusion | flops 531824640 | bytes 21174276 | tf_op jit(solution)/shard_map/while/body/eval_jaxpr/hqk,qhd->khd/dot_general | solution.py:98
  515.5 15.0 %multiply_reduce_fusion.3 = (f32[3,512]{1,0:T(4,128)S(1)}, f32[3,512,2560]{2,1,0:T(8,128)}) fusion(f32[3,512,2560]{2,1,0:T(8,128)S(1)} %fusion.137, f32[3,512]{1,0:T(4,128)S(1)} %dynamic-slice_bitcast_fusion.2, pred[512,2560]{1,0:T(8,128)(4,1)S(1)} %or_and_fusion.5, bf16[2560,3,64]{0,2,1:T(8,128)(2,1)S(1)} %copy-done.12, ...), kind=kOutput, calls=%fused_computation.19.clone.1 | convolution fusion | flops 534772224 | bytes 33959940 | tf_op jit(solution)/shard_map/while/body/eval_jaxpr/qhd,khd->hqk/dot_general | solution.py:101
  530.6 15.2 %subtract_convert_fusion.2 = bf16[3,512,2560]{2,1,0:T(8,128)(2,1)S(1)} fusion(f32[3,512,2560]{2,1,0:T(8,128)} %get-tuple-element.433, f32[3,512,2560]{2,1,0:T(8,128)} %copy-done, f32[3,512]{1,0:T(4,128)S(1)} %get-tuple-element.434, f32[3,512]{1,0:T(4,128)S(1)} %dynamic-slice_bitcast_fusion.2, pred[512,2560]{1,0:T(8,128)(4,1)S(1)} %or_and_fusion.5), kind=kLoop, calls=%fused_computation.18.clone.1 | loop fusion | flops 39321600 | bytes 40644608 | tf_op jit(solution)/shard_map/while/body/eval_jaxpr/convert_element_type | solution.py:105
  551.2 8.6 dynamic_update_slice.23
  566.2 14.4 %fusion.139 = f32[2560,3,64]{0,2,1:T(8,128)} fusion(f32[3,512,2560]{2,1,0:T(8,128)S(1)} %fusion.137, f32[3,512]{1,0:T(4,128)S(1)} %dynamic-slice_bitcast_fusion.2, pred[512,2560]{1,0:T(8,128)(4,1)S(1)} %or_and_fusion.5, f32[2560,3,64]{0,2,1:T(8,128)} %get-tuple-element.492, pred[]{:T(512)S(6)} %compare.3, ...), kind=kOutput, calls=%fused_computation.30.clone.1 | convolution fusion | flops 531824640 | bytes 21174276 | tf_op jit(solution)/shard_map/while/body/eval_jaxpr/hqk,qhd->khd/dot_general | solution.py:98
  580.6 15.0 %multiply_reduce_fusion.3 = (f32[3,512]{1,0:T(4,128)S(1)}, f32[3,512,2560]{2,1,0:T(8,128)}) fusion(f32[3,512,2560]{2,1,0:T(8,128)S(1)} %fusion.137, f32[3,512]{1,0:T(4,128)S(1)} %dynamic-slice_bitcast_fusion.2, pred[512,2560]{1,0:T(8,128)(4,1)S(1)} %or_and_fusion.5, bf16[2560,3,64]{0,2,1:T(8,128)(2,1)S(1)} %copy-done.12, ...), kind=kOutput, calls=%fused_computation.19.clone.1 | convolution fusion | flops 534772224 | bytes 33959940 | tf_op jit(solution)/shard_map/while/body/eval_jaxpr/qhd,khd->hqk/dot_general | solution.py:101
  595.7 15.2 %subtract_convert_fusion.2 = bf16[3,512,2560]{2,1,0:T(8,128)(2,1)S(1)} fusion(f32[3,512,2560]{2,1,0:T(8,128)} %get-tuple-element.433, f32[3,512,2560]{2,1,0:T(8,128)} %copy-done, f32[3,512]{1,0:T(4,128)S(1)} %get-tuple-element.434, f32[3,512]{1,0:T(4,128)S(1)} %dynamic-slice_bitcast_fusion.2, pred[512,2560]{1,0:T(8,128)(4,1)S(1)} %or_and_fusion.5), kind=kLoop, calls=%fused_computation.18.clone.1 | loop fusion | flops 39321600 | bytes 40644608 | tf_op jit(solution)/shard_map/while/body/eval_jaxpr/convert_element_type | solution.py:105
  616.2 8.6 dynamic_update_slice.23
  631.3 14.4 %fusion.139 = f32[2560,3,64]{0,2,1:T(8,128)} fusion(f32[3,512,2560]{2,1,0:T(8,128)S(1)} %fusion.137, f32[3,512]{1,0:T(4,128)S(1)} %dynamic-slice_bitcast_fusion.2, pred[512,2560]{1,0:T(8,128)(4,1)S(1)} %or_and_fusion.5, f32[2560,3,64]{0,2,1:T(8,128)} %get-tuple-element.492, pred[]{:T(512)S(6)} %compare.3, ...), kind=kOutput, calls=%fused_computation.30.clone.1 | convolution fusion | flops 531824640 | bytes 21174276 | tf_op jit(solution)/shard_map/while/body/eval_jaxpr/hqk,qhd->khd/dot_general | solution.py:98
  645.7 15.0 %multiply_reduce_fusion.3 = (f32[3,512]{1,0:T(4,128)S(1)}, f32[3,512,2560]{2,1,0:T(8,128)}) fusion(f32[3,512,2560]{2,1,0:T(8,128)S(1)} %fusion.137, f32[3,512]{1,0:T(4,128)S(1)} %dynamic-slice_bitcast_fusion.2, pred[512,2560]{1,0:T(8,128)(4,1)S(1)} %or_and_fusion.5, bf16[2560,3,64]{0,2,1:T(8,128)(2,1)S(1)} %copy-done.12, ...), kind=kOutput, calls=%fused_computation.19.clone.1 | convolution fusion | flops 534772224 | bytes 33959940 | tf_op jit(solution)/shard_map/while/body/eval_jaxpr/qhd,khd->hqk/dot_general | solution.py:101
  660.7 15.2 %subtract_convert_fusion.2 = bf16[3,512,2560]{2,1,0:T(8,128)(2,1)S(1)} fusion(f32[3,512,2560]{2,1,0:T(8,128)} %get-tuple-element.433, f32[3,512,2560]{2,1,0:T(8,128)} %copy-done, f32[3,512]{1,0:T(4,128)S(1)} %get-tuple-element.434, f32[3,512]{1,0:T(4,128)S(1)} %dynamic-slice_bitcast_fusion.2, pred[512,2560]{1,0:T(8,128)(4,1)S(1)} %or_and_fusion.5), kind=kLoop, calls=%fused_computation.18.clone.1 | loop fusion | flops 39321600 | bytes 40644608 | tf_op jit(solution)/shard_map/while/body/eval_jaxpr/convert_element_type | solution.py:105
  681.3 8.6 dynamic_update_slice.23
  696.4 14.4 %fusion.139 = f32[2560,3,64]{0,2,1:T(8,128)} fusion(f32[3,512,2560]{2,1,0:T(8,128)S(1)} %fusion.137, f32[3,512]{1,0:T(4,128)S(1)} %dynamic-slice_bitcast_fusion.2, pred[512,2560]{1,0:T(8,128)(4,1)S(1)} %or_and_fusion.5, f32[2560,3,64]{0,2,1:T(8,128)} %get-tuple-element.492, pred[]{:T(512)S(6)} %compare.3, ...), kind=kOutput, calls=%fused_computation.30.clone.1 | convolution fusion | flops 531824640 | bytes 21174276 | tf_op jit(solution)/shard_map/while/body/eval_jaxpr/hqk,qhd->khd/dot_general | solution.py:98
  710.8 15.0 %multiply_reduce_fusion.3 = (f32[3,512]{1,0:T(4,128)S(1)}, f32[3,512,2560]{2,1,0:T(8,128)}) fusion(f32[3,512,2560]{2,1,0:T(8,128)S(1)} %fusion.137, f32[3,512]{1,0:T(4,128)S(1)} %dynamic-slice_bitcast_fusion.2, pred[512,2560]{1,0:T(8,128)(4,1)S(1)} %or_and_fusion.5, bf16[2560,3,64]{0,2,1:T(8,128)(2,1)S(1)} %copy-done.12, ...), kind=kOutput, calls=%fused_computation.19.clone.1 | convolution fusion | flops 534772224 | bytes 33959940 | tf_op jit(solution)/shard_map/while/body/eval_jaxpr/qhd,khd->hqk/dot_general | solution.py:101
  725.8 15.2 %subtract_convert_fusion.2 = bf16[3,512,2560]{2,1,0:T(8,128)(2,1)S(1)} fusion(f32[3,512,2560]{2,1,0:T(8,128)} %get-tuple-element.433, f32[3,512,2560]{2,1,0:T(8,128)} %copy-done, f32[3,512]{1,0:T(4,128)S(1)} %get-tuple-element.434, f32[3,512]{1,0:T(4,128)S(1)} %dynamic-slice_bitcast_fusion.2, pred[512,2560]{1,0:T(8,128)(4,1)S(1)} %or_and_fusion.5), kind=kLoop, calls=%fused_computation.18.clone.1 | loop fusion | flops 39321600 | bytes 40644608 | tf_op jit(solution)/shard_map/while/body/eval_jaxpr/convert_element_type | solution.py:105
  746.4 8.6 dynamic_update_slice.23
  761.4 14.4 %fusion.139 = f32[2560,3,64]{0,2,1:T(8,128)} fusion(f32[3,512,2560]{2,1,0:T(8,128)S(1)} %fusion.137, f32[3,512]{1,0:T(4,128)S(1)} %dynamic-slice_bitcast_fusion.2, pred[512,2560]{1,0:T(8,128)(4,1)S(1)} %or_and_fusion.5, f32[2560,3,64]{0,2,1:T(8,128)} %get-tuple-element.492, pred[]{:T(512)S(6)} %compare.3, ...), kind=kOutput, calls=%fused_computation.30.clone.1 | convolution fusion | flops 531824640 | bytes 21174276 | tf_op jit(solution)/shard_map/while/body/eval_jaxpr/hqk,qhd->khd/dot_general | solution.py:98
  775.8 15.0 %multiply_reduce_fusion.3 = (f32[3,512]{1,0:T(4,128)S(1)}, f32[3,512,2560]{2,1,0:T(8,128)}) fusion(f32[3,512,2560]{2,1,0:T(8,128)S(1)} %fusion.137, f32[3,512]{1,0:T(4,128)S(1)} %dynamic-slice_bitcast_fusion.2, pred[512,2560]{1,0:T(8,128)(4,1)S(1)} %or_and_fusion.5, bf16[2560,3,64]{0,2,1:T(8,128)(2,1)S(1)} %copy-done.12, ...), kind=kOutput, calls=%fused_computation.19.clone.1 | convolution fusion | flops 534772224 | bytes 33959940 | tf_op jit(solution)/shard_map/while/body/eval_jaxpr/qhd,khd->hqk/dot_general | solution.py:101
  790.9 15.2 %subtract_convert_fusion.2 = bf16[3,512,2560]{2,1,0:T(8,128)(2,1)S(1)} fusion(f32[3,512,2560]{2,1,0:T(8,128)} %get-tuple-element.433, f32[3,512,2560]{2,1,0:T(8,128)} %copy-done, f32[3,512]{1,0:T(4,128)S(1)} %get-tuple-element.434, f32[3,512]{1,0:T(4,128)S(1)} %dynamic-slice_bitcast_fusion.2, pred[512,2560]{1,0:T(8,128)(4,1)S(1)} %or_and_fusion.5), kind=kLoop, calls=%fused_computation.18.clone.1 | loop fusion | flops 39321600 | bytes 40644608 | tf_op jit(solution)/shard_map/while/body/eval_jaxpr/convert_element_type | solution.py:105
  811.4 8.6 dynamic_update_slice.23
  833.5 9.9 convolution_convert_fusion.1
  843.5 8.1 fusion.76
  851.8 9.6 fusion.73
  861.6 7.8 fusion.44
  877.4 37.1 %all-reduce.8 = (f32[768]{0:T(1024)S(1)}, f32[768]{0:T(1024)S(1)}, f32[768]{0:T(1024)S(1)}, f32[768]{0:T(1024)S(1)}) all-reduce(f32[768]{0:T(1024)S(1)} %get-tuple-element.224, f32[768]{0:T(1024)S(1)} %get-tuple-element.229, f32[768]{0:T(1024)S(1)} %copy-done.34, ...), channel_id=10, replica_groups=mesh['dp'=8,'tensor'=4] {'dp'}, use_global_device_ids=true, to_apply=%region_26.27.clone | all-reduce | flops 3072 | bytes 24576
  914.7 6.5 all-reduce.9
  925.4 69.1 %reduce-scatter.21.cloned.1.call-done = f32[96,768]{1,0:T(8,128)} async-done(((f32[768,768]{1,0:T(8,128)}), f32[96,768]{1,0:T(8,128)}) %reduce-scatter.21.cloned.1.call-update) | async-done | bytes 294928 | tf_op jit(solution)/shard_map/reduce_scatter | solution.py:218
  994.5 72.9 %reduce-scatter.23.cloned.1.call-done = f32[768,96]{0,1:T(8,128)} async-done(((f32[768,768]{0,1:T(8,128)}), f32[768,96]{0,1:T(8,128)}) %reduce-scatter.23.cloned.1.call-update) | async-done | bytes 294928 | tf_op jit(solution)/shard_map/reduce_scatter | solution.py:219
  1067.4 73.3 %reduce-scatter.19.cloned.1.call-done = f32[96,3,192]{2,0,1:T(8,128)} async-done(((f32[768,3,192]{2,0,1:T(8,128)}), f32[96,3,192]{2,0,1:T(8,128)}) %reduce-scatter.19.cloned.1.call-update) | async-done | bytes 221200 | tf_op jit(solution)/shard_map/reduce_scatter | solution.py:216
  (300 shorter events, 193.8 us)
Async XLA Ops:
  8.0 35.1 %copy-start.40 = (s32[1,8]{1,0:T(1,128)S(1)}, s32[1,8]{1,0:T(1,128)}, u32[]{:S(2)}) copy-start(s32[1,8]{1,0:T(1,128)} %param.17) | copy-start | bytes 100
  8.0 35.3 %copy-start.29 = (bf16[192,96]{1,0:T(8,128)(2,1)S(1)}, bf16[192,96]{1,0:T(8,128)(2,1)}, u32[]{:S(2)}) copy-start(bf16[192,96]{1,0:T(8,128)(2,1)} %param.19) | copy-start | bytes 110596
  8.0 35.4 %copy-start.16 = (bf16[96,3,192]{2,0,1:T(8,128)(2,1)S(1)}, bf16[96,3,192]{2,0,1:T(8,128)(2,1)}, u32[]{:S(2)}) copy-start(bf16[96,3,192]{2,0,1:T(8,128)(2,1)} %param.18) | copy-start | bytes 331780
  8.0 105.5 %all-gather.6.cloned.1.call-start = ((), (), s32[]{:S(2)}) async-start(), calls=%async_computation.9 | async-start | bytes 4915200 | tf_op jit(solution)/shard_map/all_gather | solution.py:153
  43.0 246.8 %reduce-scatter.11.cloned.1.call-start = ((), (), s32[]{:S(2)}) async-start(), calls=%async_computation.10 | async-start | bytes 4915200 | tf_op jit(solution)/shard_map/reduce_scatter | solution.py:161
  80.0 38.2 %copy-start.14 = (bf16[768,3,192]{0,2,1:T(8,128)(2,1)}, bf16[768,3,192]{0,2,1:T(8,128)(2,1)S(1)}, u32[]{:S(2)}) copy-start(bf16[768,3,192]{0,2,1:T(8,128)(2,1)S(1)} %copy.33) | copy-start | bytes 2654212
  247.1 42.7 %copy-start.1 = (bf16[640,768]{1,0:T(8,128)(2,1)S(1)}, bf16[640,768]{1,0:T(8,128)(2,1)}, u32[]{:S(2)}) copy-start(bf16[640,768]{1,0:T(8,128)(2,1)} %param.15) | copy-start | bytes 2949124
  247.1 54.2 %all-gather.10.cloned.1.call-start = ((), (), s32[]{:S(2)}) async-start(), calls=%async_computation.12 | async-start | bytes 1327104 | tf_op jit(solution)/shard_map/all_gather | solution.py:135
  247.7 94.0 %all-gather.12.cloned.1.call-start = ((), (), s32[]{:S(2)}) async-start(), calls=%async_computation.14 | async-start | bytes 4915200 | tf_op jit(solution)/shard_map/all_gather | solution.py:183
  248.3 201.5 %copy-start.21 = (f32[768]{0:T(1024)}, f32[768]{0:T(1024)S(1)}, u32[]{:S(2)}) copy-start(f32[768]{0:T(1024)S(1)} %convert_element_type.109) | copy-start | bytes 9220
  291.4 158.4 %copy-start.17 = (f32[640]{0:T(1024)}, f32[640]{0:T(1024)S(1)}, u32[]{:S(2)}) copy-start(f32[640]{0:T(1024)S(1)} %broadcast_multiply_fusion.4) | copy-start | bytes 7684
  293.1 156.7 %copy-start.23 = (f32[640]{0:T(1024)}, f32[640]{0:T(1024)S(1)}, u32[]{:S(2)}) copy-start(f32[640]{0:T(1024)S(1)} %add_rsqrt_fusion) | copy-start | bytes 7684
  295.8 89.4 %all-to-all-start = ((bf16[4,640,768]{2,1,0:T(8,128)(2,1)}), bf16[4,640,768]{2,1,0:T(8,128)(2,1)}, u32[]{:S(2)}, u32[]{:S(2)}) async-start(bf16[4,640,768]{2,1,0:T(8,128)(2,1)} %stack.16), calls=%async_computation.1 | async-start | bytes 7864320 | tf_op jit(solution)/shard_map/all_to_all | solution.py:170
  300.7 84.5 %all-gather.8.cloned.1.call-start = ((), (), s32[]{:S(2)}) async-start(), calls=%async_computation.11 | async-start | bytes 1327104 | tf_op jit(solution)/shard_map/all_gather | solution.py:134
  301.3 145.7 %reduce-scatter.15.cloned.1.call-start = ((), (), s32[]{:S(2)}) async-start(), calls=%async_computation.15 | async-start | bytes 4915200 | tf_op jit(solution)/shard_map/reduce_scatter | solution.py:189
  385.2 15.8 %copy-start.39 = (bf16[768,768]{1,0:T(8,128)(2,1)S(1)}, bf16[768,768]{1,0:T(8,128)(2,1)}, u32[]{:S(2)}) copy-start(bf16[768,768]{1,0:T(8,128)(2,1)} %all-gather.8.cloned.1.call-done) | copy-start | bytes 3538948
  405.7 81.2 %all-gather.14.cloned.1.call-start = ((), (), s32[]{:S(2)}) async-start(), calls=%async_computation.16 | async-start | bytes 4915200 | tf_op jit(solution)/shard_map/all_gather | solution.py:196
  453.8 416.4 %reduce-scatter.25.cloned.1.call-start = ((), (), s32[]{:S(2)}) async-start(), calls=%async_computation.21 | async-start | bytes 884736
  491.9 383.2 %reduce-scatter.17.cloned.1.call-start = ((), (), s32[]{:S(2)}) async-start(), calls=%async_computation.17 | async-start | bytes 4915200 | tf_op jit(solution)/shard_map/reduce_scatter | solution.py:209
  503.3 12.2 %copy-start = (f32[3,512,2560]{2,1,0:T(8,128)}, f32[3,512,2560]{2,1,0:T(8,128)S(1)}, u32[]{:S(2)}) copy-start(f32[3,512,2560]{2,1,0:T(8,128)S(1)} %fusion.137) | copy-start | bytes 47185924 | tf_op jit(solution)/shard_map/while
  503.3 12.2 %copy-start.12 = (bf16[2560,3,64]{0,2,1:T(8,128)(2,1)S(1)}, bf16[2560,3,64]{0,2,1:T(8,128)(2,1)}, u32[]{:S(2)}) copy-start(bf16[2560,3,64]{0,2,1:T(8,128)(2,1)} %get-tuple-element.517) | copy-start | bytes 2949124 | tf_op jit(solution)/shard_map/while
  550.8 9.0 copy-start.4
  566.2 14.4 %copy-start = (f32[3,512,2560]{2,1,0:T(8,128)}, f32[3,512,2560]{2,1,0:T(8,128)S(1)}, u32[]{:S(2)}) copy-start(f32[3,512,2560]{2,1,0:T(8,128)S(1)} %fusion.137) | copy-start | bytes 47185924 | tf_op jit(solution)/shard_map/while
  566.2 14.4 %copy-start.12 = (bf16[2560,3,64]{0,2,1:T(8,128)(2,1)S(1)}, bf16[2560,3,64]{0,2,1:T(8,128)(2,1)}, u32[]{:S(2)}) copy-start(bf16[2560,3,64]{0,2,1:T(8,128)(2,1)} %get-tuple-element.517) | copy-start | bytes 2949124 | tf_op jit(solution)/shard_map/while
  615.9 9.0 copy-start.4
  631.3 14.4 %copy-start = (f32[3,512,2560]{2,1,0:T(8,128)}, f32[3,512,2560]{2,1,0:T(8,128)S(1)}, u32[]{:S(2)}) copy-start(f32[3,512,2560]{2,1,0:T(8,128)S(1)} %fusion.137) | copy-start | bytes 47185924 | tf_op jit(solution)/shard_map/while
  631.3 14.4 %copy-start.12 = (bf16[2560,3,64]{0,2,1:T(8,128)(2,1)S(1)}, bf16[2560,3,64]{0,2,1:T(8,128)(2,1)}, u32[]{:S(2)}) copy-start(bf16[2560,3,64]{0,2,1:T(8,128)(2,1)} %get-tuple-element.517) | copy-start | bytes 2949124 | tf_op jit(solution)/shard_map/while
  681.0 9.0 copy-start.4
  696.3 14.4 %copy-start = (f32[3,512,2560]{2,1,0:T(8,128)}, f32[3,512,2560]{2,1,0:T(8,128)S(1)}, u32[]{:S(2)}) copy-start(f32[3,512,2560]{2,1,0:T(8,128)S(1)} %fusion.137) | copy-start | bytes 47185924 | tf_op jit(solution)/shard_map/while
  696.4 14.4 %copy-start.12 = (bf16[2560,3,64]{0,2,1:T(8,128)(2,1)S(1)}, bf16[2560,3,64]{0,2,1:T(8,128)(2,1)}, u32[]{:S(2)}) copy-start(bf16[2560,3,64]{0,2,1:T(8,128)(2,1)} %get-tuple-element.517) | copy-start | bytes 2949124 | tf_op jit(solution)/shard_map/while
  746.0 9.0 copy-start.4
  761.4 14.4 %copy-start = (f32[3,512,2560]{2,1,0:T(8,128)}, f32[3,512,2560]{2,1,0:T(8,128)S(1)}, u32[]{:S(2)}) copy-start(f32[3,512,2560]{2,1,0:T(8,128)S(1)} %fusion.137) | copy-start | bytes 47185924 | tf_op jit(solution)/shard_map/while
  761.4 14.4 %copy-start.12 = (bf16[2560,3,64]{0,2,1:T(8,128)(2,1)S(1)}, bf16[2560,3,64]{0,2,1:T(8,128)(2,1)}, u32[]{:S(2)}) copy-start(bf16[2560,3,64]{0,2,1:T(8,128)(2,1)} %get-tuple-element.517) | copy-start | bytes 2949124 | tf_op jit(solution)/shard_map/while
  832.3 88.9 %reduce-scatter.13.cloned.1.call-start = ((), (), s32[]{:S(2)}) async-start(), calls=%async_computation.13 | async-start | bytes 4915200 | tf_op jit(solution)/shard_map/reduce_scatter | solution.py:176
  843.4 151.1 %reduce-scatter.21.cloned.1.call-start = ((), (), s32[]{:S(2)}) async-start(), calls=%async_computation.19 | async-start | bytes 2654208 | tf_op jit(solution)/shard_map/reduce_scatter | solution.py:218
  851.6 215.9 %reduce-scatter.23.cloned.1.call-start = ((), (), s32[]{:S(2)}) async-start(), calls=%async_computation.20 | async-start | bytes 2654208 | tf_op jit(solution)/shard_map/reduce_scatter | solution.py:219
  861.5 279.2 %reduce-scatter.19.cloned.1.call-start = ((), (), s32[]{:S(2)}) async-start(), calls=%async_computation.18 | async-start | bytes 2654208 | tf_op jit(solution)/shard_map/reduce_scatter | solution.py:216
  861.5 13.6 %copy-start.2 = (bf16[640,768]{1,0:T(8,128)(2,1)S(1)}, bf16[640,768]{1,0:T(8,128)(2,1)}, u32[]{:S(2)}) copy-start(bf16[640,768]{1,0:T(8,128)(2,1)} %param.15) | copy-start | bytes 2949124
  861.5 13.6 %copy-start.20 = (f32[640]{0:T(1024)S(1)}, f32[640]{0:T(1024)}, u32[]{:S(2)}) copy-start(f32[640]{0:T(1024)} %copy-done.19) | copy-start | bytes 7684
  861.5 13.6 %copy-start.26 = (f32[768]{0:T(1024)S(1)}, f32[768]{0:T(1024)}, u32[]{:S(2)}) copy-start(f32[768]{0:T(1024)} %copy-done.25) | copy-start | bytes 9220
  861.5 13.6 %copy-start.28 = (f32[640]{0:T(1024)S(1)}, f32[640]{0:T(1024)}, u32[]{:S(2)}) copy-start(f32[640]{0:T(1024)} %copy-done.27) | copy-start | bytes 7684
  869.3 51.9 %copy-start.6 = (bf16[640,768]{1,0:T(8,128)(2,1)S(1)}, bf16[640,768]{1,0:T(8,128)(2,1)}, u32[]{:S(2)}) copy-start(bf16[640,768]{1,0:T(8,128)(2,1)} %reduce-scatter.11.cloned.1.call-done) | copy-start | bytes 2949124
  869.3 51.9 %copy-start.7 = (bf16[640,768]{1,0:T(8,128)(2,1)S(1)}, bf16[640,768]{1,0:T(8,128)(2,1)}, u32[]{:S(2)}) copy-start(bf16[640,768]{1,0:T(8,128)(2,1)} %param.16) | copy-start | bytes 2949124
  869.3 51.9 %copy-start.18 = (f32[640]{0:T(1024)S(1)}, f32[640]{0:T(1024)}, u32[]{:S(2)}) copy-start(f32[640]{0:T(1024)} %copy-done.17) | copy-start | bytes 7684
  869.3 51.9 %copy-start.22 = (f32[768]{0:T(1024)S(1)}, f32[768]{0:T(1024)}, u32[]{:S(2)}) copy-start(f32[768]{0:T(1024)} %copy-done.21) | copy-start | bytes 9220
  869.3 51.9 %copy-start.24 = (f32[640]{0:T(1024)S(1)}, f32[640]{0:T(1024)}, u32[]{:S(2)}) copy-start(f32[640]{0:T(1024)} %copy-done.23) | copy-start | bytes 7684
  869.4 51.9 %copy-start.31 = (f32[640]{0:T(1024)S(1)}, f32[640]{0:T(1024)}, u32[]{:S(2)}) copy-start(f32[640]{0:T(1024)} %copy-done.30) | copy-start | bytes 7684
  869.4 51.9 %copy-start.33 = (f32[640]{0:T(1024)S(1)}, f32[640]{0:T(1024)}, u32[]{:S(2)}) copy-start(f32[640]{0:T(1024)} %copy-done.32) | copy-start | bytes 7684
  (24 other events, 72.5 us)
Sparse Core Ops, SparseCore 0:
  43.1 30.2 all-gather.5
  247.3 42.4 reduce-scatter.10
  453.9 32.9 all-gather.13
Sparse Core Ops, SparseCore 1:
  249.8 41.0 all-gather.9
  292.3 49.4 all-gather.11
  343.7 41.4 all-gather.7
  405.8 41.1 reduce-scatter.14
  492.0 63.3 reduce-scatter.24
  832.3 42.8 reduce-scatter.16
  877.6 42.8 reduce-scatter.12
  924.3 70.1 reduce-scatter.20
  998.4 68.9 reduce-scatter.22
  1071.5 69.1 reduce-scatter.18
